TPU v7x, 32 devices: a whole 2x2x4 slice. The times are simulated.
32 devices in a mesh: mol: 8 (over y, x, core), grid: 4 (over z).
Axes of the slice: x: 2, y: 2, z: 4, core: 2. Of those that a mesh axis runs over, the one named last changes fastest.
Arguments:
- cells_start: int32 [65536], P('mol'), may hold values from 0 to 524287
- moves: int32 [2, 3, 65536], P(None, None, 'mol'), may hold values from -1 to 1
- accepted: int32 [2, 65536], P(None, 'mol'), may hold values from 0 to 1
- bead_types: int32 [65536], P('mol'), may hold values from 0 to 1
Outputs:
- energy_change: float32 [2, 65536], P(None, 'mol')
- final_field: bfloat16 [64, 16, 1024], P('mol', 'grid')
All inputs are finite; a program needn't handle non-finite values.
Results may differ from a plain program's by a relative error of at most 0.0048.
Values may be sent and summed in bfloat16 or wider, within the bound.
A program may use at most 64 MiB of HBM per device.

v0:
```python
import jax
import jax.numpy as jnp
from jax import lax
from jax.sharding import PartitionSpec as P

NX = 512
NY = 64
ZDEV = 4
STEPS = 2
SPREAD = 2


chi_mix = 1.0
kappa_comp = 0.5


def kernel_rows(col_x):
    column = jnp.arange(NX, dtype=jnp.float32)
    distance = jnp.abs(column[None, :] - col_x.astype(jnp.float32)[:, None])
    distance = jnp.minimum(distance, NX - distance)
    weights = jnp.exp(-distance * distance / (2.0 * SPREAD * SPREAD))
    first = jnp.abs(column)
    first = jnp.minimum(first, NX - first)
    total = jnp.sum(jnp.exp(-first * first / (2.0 * SPREAD * SPREAD)))
    return (weights / total).astype(jnp.bfloat16)


def split_cell(cells):
    col_x = cells % NX
    row_y = cells // NX % NY
    plane_z = cells // (NX * NY)
    return (col_x, row_y, plane_z)


def move_cells(cells, shift, planes):
    col_x, row_y, plane_z = split_cell(cells)
    col_x = (col_x + shift[0]) % NX
    row_y = (row_y + shift[1]) % NY
    plane_z = (plane_z + shift[2]) % planes
    return (plane_z * NY + row_y) * NX + col_x


def deposit(positions, bead_types, slab, start, count):
    col_x, row_y, plane_z = split_cell(positions)
    inside = (plane_z // ZDEV == slab) & (row_y >= start) & (row_y < start + count)
    row_id = jnp.where(inside, row_y * ZDEV + plane_z - slab * ZDEV, -1)
    bead_count = positions.shape[0]
    block_size = min(1024, bead_count)
    row_total = count * ZDEV
    targets = lax.broadcasted_iota(jnp.int32, (row_total, block_size), 0)

    def add_block(block_id, total):
        begin = block_id * block_size
        rows_here = lax.dynamic_slice_in_dim(row_id, begin, block_size)
        cols_here = lax.dynamic_slice_in_dim(col_x, begin, block_size)
        types_here = lax.dynamic_slice_in_dim(bead_types, begin, block_size)
        onehot = (rows_here[None, :] == targets).astype(jnp.bfloat16)
        spread_rows = kernel_rows(cols_here)
        zeros_bf = jnp.zeros_like(spread_rows)
        first = jnp.where(types_here[:, None] == 0, spread_rows, zeros_bf)
        second = jnp.where(types_here[:, None] == 1, spread_rows, zeros_bf)
        columns = jnp.concatenate([first, second], axis=1)
        return total + jnp.dot(onehot, columns, preferred_element_type=jnp.float32)

    empty = jnp.zeros((row_total, 2 * NX), jnp.float32)
    total = lax.fori_loop(0, bead_count // block_size, add_block, empty)
    return total.reshape(count, ZDEV, 2 * NX)


def make_field(density):
    phi_a = density[:, :, :NX]
    phi_b = density[:, :, NX:]
    excess = kappa_comp * (phi_a + phi_b - 1.0)
    field_a = chi_mix * phi_b + excess
    field_b = chi_mix * phi_a + excess
    return jnp.concatenate([field_a, field_b], axis=2).astype(jnp.bfloat16)


def make_reader(points, bead_types, z_first, z_span):
    col_x, row_y, plane_z = split_cell(points)
    local_z = plane_z - z_first
    kinds = jnp.broadcast_to(bead_types[None, :], points.shape)
    column_id = kinds * NX + col_x

    def read_beads(carry, piece, start):
        span_rows = piece.shape[0]
        flat_table = piece.reshape(-1)
        valid = (row_y >= 0) & (row_y < span_rows) & (local_z >= 0) & (local_z < z_span)
        flat_index = jnp.where(valid, (row_y * z_span + local_z) * (2 * NX) + column_id, 0)
        picked = jnp.take(flat_table, flat_index).astype(jnp.float32)
        return jnp.where(valid, picked, 0.0)

    return read_beads


def local(cells_start, moves, accepted, bead_types):
    grid_count = lax.axis_size("grid")
    mol_count = lax.axis_size("mol")
    slab = lax.axis_index("grid")
    planes = ZDEV * grid_count
    bead_count = cells_start.shape[0]
    scale = NX * NY * planes / (bead_count * mol_count)
    band_rows = NY // mol_count
    positions = [cells_start]
    proposals = []
    for step in range(STEPS):
        proposed = move_cells(positions[step], moves[step], planes)
        proposals.append(proposed)
        positions.append(jnp.where(accepted[step] == 1, proposed, positions[step]))
    fields = []

    def both_terms(start):
        return jnp.concatenate(
            [
                deposit(positions[step], bead_types, slab, start, lax.axis_size("mol") * band_rows)
                for step in range(STEPS)
            ],
            axis=1,
        )

    summed = lax.psum_scatter(both_terms(jnp.int32(0)), "mol", scatter_dimension=0, tiled=True)
    for step in range(STEPS):
        fields.append(make_field(scale * summed[:, step * ZDEV : (step + 1) * ZDEV, :]))
    changes = []
    for step in range(STEPS):
        points = jnp.stack([positions[step], proposals[step]])
        start_values = jnp.zeros(points.shape, jnp.float32)
        whole_z = lax.all_gather(fields[step], "grid", axis=1, tiled=True)
        reader = make_reader(points, bead_types, 0, planes)
        values = reader(
            start_values, lax.all_gather(whole_z, "mol", axis=0, tiled=True), jnp.int32(0)
        )
        changes.append(values[1] - values[0])
    return (jnp.stack(changes), fields[STEPS - 1])


def solution(mesh):
    return jax.shard_map(
        local,
        mesh=mesh,
        in_specs=(P("mol"), P(None, None, "mol"), P(None, "mol"), P("mol")),
        out_specs=(P(None, "mol"), P("mol", "grid", None)),
        check_vma=False,
    )
```

profile of v0, /device:TPU:0, one launch (start us, length us, event | category | flops | bytes accessed | tf_op | source)
XLA Modules:
  0.0 393.6 jit_solution(15904831323837670896)
XLA Ops:
  10.5 33.7 %while.29 = (s32[]{:T(128)}, f32[256,1024]{1,0:T(8,128)S(1)}, s32[8192]{0:T(1024)S(1)}, s32[8192]{0:T(1024)}, s32[8192]{0:T(1024)S(1)}, /*index=5*/s32[]{:T(128)}, s32[]{:T(128)}, s32[]{:T(128)}, s32[]{:T(128)}) while((s32[]{:T(128)}, f32[256,1024]{1,0:T(8,128)S(1)}, s32[8192]{0:T(1024)S(1)}, s32[8192]{0:T(1024)}, ...), condition=%wide.region_5.6_spmd.clone, body=%wide.region_3.5_spmd.clone.sunk | while | flops 547624960 | bytes 6324393 | solution.py:66
  11.9 1.9 fusion.90
  16.1 1.9 fusion.90
  20.3 1.9 fusion.90
  24.5 1.9 fusion.90
  28.7 1.9 fusion.90
  33.0 1.9 fusion.90
  37.2 1.9 fusion.90
  41.4 1.9 fusion.90
  45.0 42.3 %while.28 = (s32[]{:T(128)}, f32[256,1024]{1,0:T(8,128)}, s32[8192]{0:T(1024)S(1)}, s32[8192]{0:T(1024)S(1)}, s32[8192]{0:T(1024)S(1)}, /*index=5*/s32[]{:T(128)}, s32[]{:T(128)}, s32[]{:T(128)}, s32[]{:T(128)}) while((s32[]{:T(128)}, f32[256,1024]{1,0:T(8,128)}, s32[8192]{0:T(1024)S(1)}, s32[8192]{0:T(1024)S(1)}, ...), condition=%wide.region_2.3_spmd.clone, body=%wide.region_0.2_spmd.clone.sunk | while | flops 547624960 | bytes 6324393 | solution.py:66
  45.6 1.9 fusion.86
  49.8 1.9 fusion.86
  51.7 2.9 fusion.87
  55.3 1.9 fusion.86
  57.2 2.9 fusion.87
  60.7 1.9 fusion.86
  62.6 2.9 fusion.87
  66.2 1.9 fusion.86
  68.1 2.9 fusion.87
  71.6 1.9 fusion.86
  73.5 2.9 fusion.87
  77.1 1.9 fusion.86
  78.9 2.9 fusion.87
  84.4 2.9 fusion.87
  90.8 43.9 %reduce-scatter.2.cloned.1.call-done = f32[8,8,1024]{2,1,0:T(8,128)} async-done(((f32[64,8,1024]{2,1,0:T(8,128)}), f32[8,8,1024]{2,1,0:T(8,128)}) %reduce-scatter.2.cloned.1.call-update) | async-done | bytes 262160 | tf_op jit(solution)/shard_map/reduce_scatter | solution.py:121
  135.9 13.8 %all_gather.12 = bf16[8,16,1024]{2,0,1:T(8,128)(2,1)S(1)} all-gather(bf16[8,4,1024]{2,0,1:T(8,128)(2,1)S(1)} %copy.6), channel_id=1, replica_groups=mesh['mol'=8,'grid'=4] {'grid'}, dimensions={1}, use_global_device_ids=true | all-gather | bytes 327680 | tf_op jit(solution)/shard_map/all_gather | solution.py:128
  152.0 14.6 %all_gather.14 = bf16[8,16,1024]{2,0,1:T(8,128)(2,1)S(1)} all-gather(bf16[8,4,1024]{2,0,1:T(8,128)(2,1)S(1)} %copy.8), channel_id=1, replica_groups=mesh['mol'=8,'grid'=4] {'grid'}, dimensions={1}, use_global_device_ids=true | all-gather | bytes 327680 | tf_op jit(solution)/shard_map/all_gather | solution.py:128
  167.5 11.8 %all-gather.3.cloned.1.call-done = bf16[64,16,1024]{2,1,0:T(8,128)(2,1)} async-done(((bf16[8,16,1024]{2,1,0:T(8,128)(2,1)}), bf16[64,16,1024]{2,1,0:T(8,128)(2,1)}) %all-gather.3.cloned.1.call-update) | async-done | bytes 2097168 | tf_op jit(solution)/shard_map/all_gather | solution.py:131
  179.3 2.2 copy.10
  181.5 100.9 %gather_fusion = bf16[16384]{0:T(1024)(128)(2,1)S(1)} fusion(bf16[1048576]{0:T(1024)(128)(2,1)S(1)} %bitcast.18, s32[16384]{0:T(1024)S(1)} %broadcast_clamp_fusion.1), kind=kCustom, calls=%fused_computation.clone | custom fusion | bytes 131072 | tf_op jit(solution)/shard_map/jit(_take)/gather | solution.py:90
  282.8 2.2 copy.12
  285.1 100.9 %gather_fusion.1 = bf16[16384]{0:T(1024)(128)(2,1)S(1)} fusion(bf16[1048576]{0:T(1024)(128)(2,1)S(1)} %bitcast.19, s32[16384]{0:T(1024)S(1)} %broadcast_clamp_fusion), kind=kCustom, calls=%fused_computation.1.clone | custom fusion | bytes 131072 | tf_op jit(solution)/shard_map/jit(_take)/gather | solution.py:90
  (117 shorter events, 39.9 us)
Async XLA Ops:
  7.2 127.5 %reduce-scatter.2.cloned.1.call-start = ((), (), s32[]{:S(2)}) async-start(), calls=%async_computation.1 | async-start | bytes 2359296 | tf_op jit(solution)/shard_map/reduce_scatter | solution.py:121
  44.2 0.8 copy-start.2
  90.7 60.0 %copy-start = (s32[8192]{0:T(1024)S(1)}, s32[8192]{0:T(1024)}, u32[]{:S(2)}) copy-start(s32[8192]{0:T(1024)} %param.10) | copy-start | bytes 98308
  90.7 88.6 %all-gather.3.cloned.1.call-start = ((), (), s32[]{:S(2)}) async-start(), calls=%async_computation.2 | async-start | bytes 2359296 | tf_op jit(solution)/shard_map/all_gather | solution.py:131
  150.6 132.2 %all-gather.5.cloned.1.call-start = ((), (), s32[]{:S(2)}) async-start(), calls=%async_computation.3 | async-start | bytes 2359296 | tf_op jit(solution)/shard_map/all_gather | solution.py:131
  152.0 29.5 %copy-start.1 = (bf16[8,4,1024]{2,1,0:T(4,128)(2,1)}, bf16[8,4,1024]{2,1,0:T(4,128)(2,1)S(1)}, u32[]{:S(2)}) copy-start(bf16[8,4,1024]{2,1,0:T(4,128)(2,1)S(1)} %pad_maximum_fusion.2) | copy-start | bytes 196612
Sparse Core Ops, SparseCore 0:
  90.8 43.8 reduce-scatter.1
  150.8 28.4 all-gather.2
  181.2 27.7 all-gather.4
where the time goes:
time: 395 us; the launch traced here: 394 us
  local copies, waits for them, and re-layouts  212 us (54%)
  waiting for transfers between devices  55.8 us (14%)
  other arithmetic  53.9 us (14%)
  matrix products  29 us (7%)
  blocking collectives  28.4 us (7%)
  between operations  14 us (4%)
    gather x4, local copies, waits for them, and re-layouts, read_beads(): picked = jnp.take(flat_table, flat_index).astype(jnp.float32)  202 us
    reduce_scatter x1, waiting for transfers between devices, local(): lax.psum_scatter(both_terms(jnp.int32(0)), 'mol', scatter_dimension=0, ti...  43.9 us
    select_n x16, other arithmetic, add_block(): first = jnp.where(types_here[:, None] == 0, spread_rows, zeros_bf)  30.1 us
    dot_general x16, matrix products, add_block(): return total + jnp.dot(onehot, columns, preferred_element_type=jnp.float32)  29 us
    all_gather x2, blocking collectives, local(): whole_z = lax.all_gather(fields[step], 'grid', axis=1, tiled=True)  28.4 us
    all_gather x2, waiting for transfers between devices, local(): lax.all_gather(whole_z, 'mol', axis=0, tiled=True)  11.8 us
    reduce_sum x16, other arithmetic, kernel_rows(): total = jnp.sum(jnp.exp(-first * first / (2.0 * SPREAD * SPREAD)))  10.5 us
  transfers between devices with their start and end apart: 3, of which 2 were waited for; matrix products, arithmetic and copies ran while one was open for 27% of the time, Pallas kernels for 0%

commit v1 on v0

v1 whole, which is shorter than its diff:
```python
import functools

import jax
import jax.numpy as jnp
import numpy as np
from jax import lax
from jax.experimental import pallas as pl
from jax.experimental.pallas import tpu as pltpu
from jax.sharding import PartitionSpec as P

NX = 512
NY = 64
ZDEV = 4
STEPS = 2
TYPES = 2
SPREAD = 2

chi_mix = 1.0
kappa_comp = 0.5

MESH = pl.DeviceIdType.MESH
VMEM = pltpu.MemorySpace.VMEM
LIMIT = 60 * 1024 * 1024


def kernel_table():
    column = np.arange(NX, dtype=np.float32)
    distance = np.abs(column[:, None] - column[None, :])
    distance = np.minimum(distance, NX - distance)
    weights = np.exp(-distance * distance / np.float32(2.0 * SPREAD * SPREAD))
    return (weights / np.sum(weights[0])).astype(jnp.bfloat16)


def split_cell(cells):
    return cells % NX, cells // NX % NY, cells // (NX * NY)


def onehot(ids, size):
    tile = min(256, size)
    count = lax.broadcasted_iota(jnp.int32, (tile, ids.shape[1]), 0).astype(jnp.bfloat16)
    one = jnp.ones(count.shape, jnp.bfloat16)
    zero = jnp.zeros(count.shape, jnp.bfloat16)
    tiles = []
    for start in range(0, size, tile):
        here = jnp.broadcast_to((ids - start).astype(jnp.bfloat16), count.shape)
        tiles.append(jnp.where(count == here, one, zero))
    return jnp.concatenate(tiles, axis=0) if len(tiles) > 1 else tiles[0]


def deposit_kernel(row_ref, col_ref, out_ref, total):
    block = pl.program_id(1)

    @pl.when(block == 0)
    def _():
        total[...] = jnp.zeros_like(total)

    rows = onehot(row_ref[0], total.shape[0])
    cols = onehot(col_ref[0], total.shape[1])
    total[...] += lax.dot_general(
        rows, cols, (((1,), (1,)), ((), ())), preferred_element_type=jnp.float32
    )

    @pl.when(block == pl.num_programs(1) - 1)
    def _():
        out_ref[0] = total[...].astype(jnp.bfloat16)


def deposit(rows, cols, row_total):
    beads = rows.shape[-1]
    block = min(1024, beads)
    return pl.pallas_call(
        deposit_kernel,
        grid=(STEPS, beads // block),
        out_shape=jax.ShapeDtypeStruct((STEPS, row_total, NX), jnp.bfloat16),
        in_specs=[pl.BlockSpec((1, 1, block), lambda s, b: (s, 0, b))] * 2,
        out_specs=pl.BlockSpec((1, row_total, NX), lambda s, b: (s, 0, 0)),
        scratch_shapes=[pltpu.VMEM((row_total, NX), jnp.float32)],
        compiler_params=pltpu.CompilerParams(vmem_limit_bytes=LIMIT),
        name="deposit",
    )(rows, cols)


def field_kernel(peers, scale, count_ref, table_ref, all_ref, own_ref, inbox, sums, send_a, recv_a, send_b, recv_b):
    me = lax.axis_index("mol")
    barrier = pltpu.get_barrier_semaphore()
    for away in range(1, peers):
        pl.semaphore_signal(
            barrier, inc=1, device_id={"mol": lax.rem(me + away, peers)}, device_id_type=MESH
        )
    pl.semaphore_wait(barrier, peers - 1)
    parts = {}
    for step in range(STEPS):
        for away in range(1, peers):
            to = lax.rem(me + away, peers)
            copy = pltpu.make_async_remote_copy(
                src_ref=count_ref.at[step, to],
                dst_ref=inbox.at[step, away - 1],
                send_sem=send_a.at[step, away - 1],
                recv_sem=recv_a.at[step, away - 1],
                device_id={"mol": to},
                device_id_type=MESH,
            )
            copy.start()
            parts[step, away] = copy
    half = count_ref.shape[2] // 2
    fields = {}
    for step in range(STEPS):
        total = count_ref[step, me].astype(jnp.float32)
        for away in range(1, peers):
            parts[step, away].wait_recv()
            total = total + inbox[step, away - 1].astype(jnp.float32)
        sums[...] = total
        high = sums[...].astype(jnp.bfloat16)
        low = (sums[...] - high.astype(jnp.float32)).astype(jnp.bfloat16)
        table = table_ref[...]
        density = jnp.dot(high, table, preferred_element_type=jnp.float32)
        density = scale * (density + jnp.dot(low, table, preferred_element_type=jnp.float32))
        phi_a, phi_b = density[:half], density[half:]
        excess = kappa_comp * (phi_a + phi_b - 1.0)
        field_a = (chi_mix * phi_b + excess).astype(jnp.bfloat16)
        field_b = (chi_mix * phi_a + excess).astype(jnp.bfloat16)
        all_ref[step, me, :half] = field_a
        all_ref[step, me, half:] = field_b
        if step == STEPS - 1:
            own_ref[:, :NX] = field_a
            own_ref[:, NX:] = field_b
        for away in range(1, peers):
            to = lax.rem(me + away, peers)
            copy = pltpu.make_async_remote_copy(
                src_ref=all_ref.at[step, me],
                dst_ref=all_ref.at[step, me],
                send_sem=send_b.at[step, away - 1],
                recv_sem=recv_b.at[step, away - 1],
                device_id={"mol": to},
                device_id_type=MESH,
            )
            copy.start()
            fields[step, away] = copy
    for step in range(STEPS):
        for away in range(1, peers):
            fields[step, away].wait_recv()
    for step in range(STEPS):
        for away in range(1, peers):
            parts[step, away].wait_send()
            fields[step, away].wait_send()


def make_fields(counts, table, scale):
    steps, peers, rows, _ = counts.shape
    spec = pl.BlockSpec(memory_space=VMEM)
    sems = [pltpu.SemaphoreType.DMA((steps, peers - 1))] * 4
    return pl.pallas_call(
        functools.partial(field_kernel, peers, scale),
        out_shape=[
            jax.ShapeDtypeStruct(counts.shape, jnp.bfloat16),
            jax.ShapeDtypeStruct((rows // TYPES, TYPES * NX), jnp.bfloat16),
        ],
        in_specs=[spec] * 2,
        out_specs=[spec] * 2,
        scratch_shapes=[
            pltpu.VMEM((steps, peers - 1, rows, NX), jnp.bfloat16),
            pltpu.VMEM((rows, NX), jnp.float32),
            *sems,
        ],
        compiler_params=pltpu.CompilerParams(
            collective_id=0, has_side_effects=True, vmem_limit_bytes=LIMIT
        ),
        name="fields",
    )(counts, table)


def read_kernel(rc_ref, cc_ref, rp_ref, cp_ref, field_ref, out_ref, turned):
    @pl.when(pl.program_id(1) == 0)
    def _():
        size = turned.shape[0]
        eye = (
            lax.broadcasted_iota(jnp.int32, (size, size), 0)
            == lax.broadcasted_iota(jnp.int32, (size, size), 1)
        )
        eye = jnp.where(eye, 1.0, 0.0).astype(jnp.bfloat16)
        turned[...] = lax.dot_general(
            eye, field_ref[0], (((1,), (1,)), ((), ())), preferred_element_type=jnp.float32
        ).astype(jnp.bfloat16)

    table = turned[...]

    def pick(rows, cols):
        values = jnp.dot(table, onehot(rows, table.shape[1]), preferred_element_type=jnp.float32)
        columns = lax.broadcasted_iota(jnp.int32, values.shape, 0)
        return jnp.sum(jnp.where(columns == cols, values, 0.0), axis=0, keepdims=True)

    out_ref[0] = pick(rp_ref[0], cp_ref[0]) - pick(rc_ref[0], cc_ref[0])


def read(rows, cols, rows_p, cols_p, field):
    beads = rows.shape[-1]
    block = min(1024, beads)
    spec = pl.BlockSpec((1, 1, block), lambda s, b: (s, 0, b))
    row_total = field.shape[1]
    return pl.pallas_call(
        read_kernel,
        grid=(STEPS, beads // block),
        out_shape=jax.ShapeDtypeStruct((STEPS, 1, beads), jnp.float32),
        in_specs=[spec] * 4 + [pl.BlockSpec((1, row_total, NX), lambda s, b: (s, 0, 0))],
        out_specs=spec,
        scratch_shapes=[pltpu.VMEM((NX, row_total), jnp.bfloat16)],
        compiler_params=pltpu.CompilerParams(vmem_limit_bytes=LIMIT),
        name="read",
    )(rows, cols, rows_p, cols_p, field)


def exchange_kernel(peers, part_ref, out_ref, inbox, send, recv):
    me = lax.axis_index("grid")
    barrier = pltpu.get_barrier_semaphore()
    for away in range(1, peers):
        pl.semaphore_signal(
            barrier, inc=1, device_id={"grid": lax.rem(me + away, peers)}, device_id_type=MESH
        )
    pl.semaphore_wait(barrier, peers - 1)
    copies = []
    for away in range(1, peers):
        copy = pltpu.make_async_remote_copy(
            src_ref=part_ref,
            dst_ref=inbox.at[away - 1],
            send_sem=send.at[away - 1],
            recv_sem=recv.at[away - 1],
            device_id={"grid": lax.rem(me + away, peers)},
            device_id_type=MESH,
        )
        copy.start()
        copies.append(copy)
    total = part_ref[...]
    for away in range(1, peers):
        copies[away - 1].wait_recv()
        total = total + inbox[away - 1]
    out_ref[...] = total
    for copy in copies:
        copy.wait_send()


def exchange(part, peers):
    spec = pl.BlockSpec(memory_space=VMEM)
    return pl.pallas_call(
        functools.partial(exchange_kernel, peers),
        out_shape=jax.ShapeDtypeStruct(part.shape, jnp.float32),
        in_specs=[spec],
        out_specs=spec,
        scratch_shapes=[
            pltpu.VMEM((peers - 1, *part.shape), jnp.float32),
            pltpu.SemaphoreType.DMA((peers - 1,)),
            pltpu.SemaphoreType.DMA((peers - 1,)),
        ],
        compiler_params=pltpu.CompilerParams(
            collective_id=1, has_side_effects=True, vmem_limit_bytes=LIMIT
        ),
        name="exchange",
    )(part)


def local(cells_start, moves, accepted, bead_types):
    grid_count = lax.axis_size("grid")
    mol_count = lax.axis_size("mol")
    slab = lax.axis_index("grid")
    planes = ZDEV * grid_count
    beads = cells_start.shape[0]
    scale = NX * NY * planes / (beads * mol_count)
    band = NY // mol_count
    row_total = TYPES * NY * ZDEV

    def row_of(spot):
        _, row_y, plane_z = spot
        inside = plane_z // ZDEV == slab
        row = ((row_y // band * TYPES + bead_types) * band + row_y % band) * ZDEV
        return jnp.where(inside, row + plane_z % ZDEV, -1)

    position = split_cell(cells_start)
    spots, proposals = [], []
    for step in range(STEPS):
        lengths = (NX, NY, planes)
        proposed = tuple((position[i] + moves[step, i]) % lengths[i] for i in range(3))
        spots.append(position)
        proposals.append(proposed)
        position = tuple(
            jnp.where(accepted[step] == 1, proposed[i], position[i]) for i in range(3)
        )
    rows = jnp.stack([row_of(spot) for spot in spots])[:, None]
    cols = jnp.stack([spot[0] for spot in spots])[:, None]
    rows_p = jnp.stack([row_of(spot) for spot in proposals])[:, None]
    cols_p = jnp.stack([spot[0] for spot in proposals])[:, None]

    counts = deposit(rows, cols, row_total)
    counts = counts.reshape(STEPS, mol_count, row_total // mol_count, NX)
    fields, own = make_fields(counts, jnp.asarray(kernel_table()), scale)
    part = read(rows, cols, rows_p, cols_p, fields.reshape(STEPS, row_total, NX))
    part = part.reshape(-1, 128)
    total = exchange(part, grid_count).reshape(STEPS, beads)
    return total, own.reshape(band, ZDEV, TYPES * NX)


def solution(mesh):
    return jax.shard_map(
        local,
        mesh=mesh,
        in_specs=(P("mol"), P(None, None, "mol"), P(None, "mol"), P("mol")),
        out_specs=(P(None, "mol"), P("mol", "grid", None)),
        check_vma=False,
    )
```

time: 395 us -> 89.3 us (0.23)
  local copies, waits for them, and re-layouts: 212 us -> 6.07 us
  Pallas kernels: 0 us -> 80.4 us
  waiting for transfers between devices: 55.8 us -> 0 us
  other arithmetic: 53.9 us -> 1.56 us
  matrix products: 29 us -> 0 us
  blocking collectives: 28.4 us -> 0 us
  between operations: 14 us -> 0.72 us
    gather x4 -> x0, local copies, waits for them, and re-layouts: 202 us -> none  [read_beads(): picked = jnp.take(flat_table, flat_index).astype(jnp.float32)]
    pallas_call x0 -> x4, Pallas kernels: none -> 80.4 us  [the longest x1 30.2 us: make_fields(): pl.pallas_call(functools.partial(field_kernel, peers, scale), out_shape=[...]
    reduce_scatter x1 -> x0, waiting for transfers between devices: 43.9 us -> none  [local(): lax.psum_scatter(both_terms(jnp.int32(0)), 'mol', scatter_dimension=0, ti...]
    select_n x20 -> x1, other arithmetic: 32 us -> 0.4 us  [row_of(): return jnp.where(inside, row + plane_z % ZDEV, -1)]
    dot_general x16 -> x0, matrix products: 29 us -> none  [add_block(): return total + jnp.dot(onehot, columns, preferred_element_type=jnp.float32)]
    all_gather x2 -> x0, blocking collectives: 28.4 us -> none  [local(): whole_z = lax.all_gather(fields[step], 'grid', axis=1, tiled=True)]
    all_gather x2 -> x0, waiting for transfers between devices: 11.8 us -> none  [local(): lax.all_gather(whole_z, 'mol', axis=0, tiled=True)]
    reduce_sum x16 -> x0, other arithmetic: 10.5 us -> none  [kernel_rows(): total = jnp.sum(jnp.exp(-first * first / (2.0 * SPREAD * SPREAD)))]
  transfers between devices with their start and end apart: 3 -> 0, of which waited for: 2 -> 0; matrix products, arithmetic and copies ran while one was open for 27% -> 0% of each run, Pallas kernels for 0% -> 0%
where the time goes in v1:
time: 89.3 us; the launch traced here: 88.8 us
  Pallas kernels  80.4 us (90%)
  local copies, waits for them, and re-layouts  6.07 us (7%)
  other arithmetic  1.56 us (2%)
    pallas_call x1, Pallas kernels, make_fields(): pl.pallas_call(functools.partial(field_kernel, peers, scale), out_shape=[...  30.2 us
    pallas_call x1, Pallas kernels, read(): pl.pallas_call(read_kernel, grid=(STEPS, beads // block), out_shape=jax.S...  25.1 us
    pallas_call x1, Pallas kernels, deposit(): pl.pallas_call(deposit_kernel, grid=(STEPS, beads // block), out_shape=ja...  14.1 us
    pallas_call x1, Pallas kernels, exchange(): pl.pallas_call(functools.partial(exchange_kernel, peers), out_shape=jax.S...  11 us

profile of v1, /device:TPU:0, one launch (start us, length us, event | category | flops | bytes accessed | tf_op | source)
XLA Modules:
  0.0 88.8 jit_solution(3881122673707341701)
XLA Ops:
  0.6 0.9 %compare_reduce_fusion = pred[8192]{0:T(1024)(128)(4,1)S(1)} fusion(s32[2,8192]{1,0:T(2,128)} %param.7), kind=kLoop, calls=%fused_computation | loop fusion | flops 8192 | bytes 40960 | tf_op jit(solution)/shard_map/eq | solution.py:284
  1.6 0.0 copy-start.1
  1.6 0.0 copy-start.2
  1.6 1.2 %fusion.68 = (s32[1,1,8192]{2,0,1:T(1,128)S(1)}, s32[1,1,8192]{2,0,1:T(1,128)S(1)}, s32[1,1,8192]{2,0,1:T(1,128)S(1)}, s32[1,1,8192]{2,0,1:T(1,128)S(1)}, s32[1,...) fusion(s32[2,3,8192]{2,0,1:T(2,128)} %param.6), kind=kLoop, calls=%fused_computation.150 | loop fusion | bytes 393216 | tf_op jit(solution)/shard_map/slice | solution.py:280
  2.8 0.0 copy-done.1
  2.8 0.0 copy-done.2
  2.8 0.4 fusion.38
  3.2 0.1 pad_add_fusion.2
  3.3 0.7 broadcast_in_dim.19.rp_ref
  3.9 0.1 pad_add_fusion
  4.0 0.7 broadcast_in_dim.17.row_ref.rc_ref
  4.7 0.1 pad_add_fusion.3
  4.7 0.7 broadcast_in_dim.20.cp_ref
  5.4 0.1 pad_add_fusion.1
  5.5 0.7 broadcast_in_dim.18.col_ref.cc_ref
  6.1 14.1 %deposit.1 = bf16[2,512,512]{2,1,0:T(8,128)(2,1)} custom-call(s32[2,1,8192]{2,1,0:T(1,128)} %broadcast_in_dim.17.row_ref.rc_ref, s32[2,1,8192]{2,1,0:T(1,128)} %broadcast_in_dim.18.col_ref.cc_ref), custom_call_target="tpu_custom_call" | custom-call | tf_op jit(solution)/shard_map/deposit/pallas_call | solution.py:71
  20.3 30.2 %fields.1 = (bf16[2,8,64,512]{3,2,1,0:T(8,128)(2,1)}, bf16[32,1024]{1,0:T(8,128)(2,1)}) custom-call(bf16[2,8,64,512]{3,2,1,0:T(8,128)(2,1)} %bitcast.17, bf16[512,512]{1,0:T(8,128)(2,1)} %constant.207.clone.table_ref), custom_call_target="tpu_custom_call" | custom-call | tf_op jit(solution)/shard_map/fields/pallas_call | solution.py:152
  50.4 25.1 %read.1 = f32[2,1,8192]{2,1,0:T(1,128)} custom-call(s32[2,1,8192]{2,1,0:T(1,128)} %broadcast_in_dim.17.row_ref.rc_ref, s32[2,1,8192]{2,1,0:T(1,128)} %broadcast_in_dim.18.col_ref.cc_ref, s32[2,1,8192]{2,1,0:T(1,128)} %broadcast_in_dim.19.rp_ref, s32[2,1,8192]{2,1,0:T(1,128)} %broadcast_in_dim.20.cp_ref, bf16[2,512,512]{2,1,0:T(8,128)(2,1)} %bitcast.18), custom_call_target="tpu_custom_call" | custom-call | tf_op jit(solution)/shard_map/read/pallas_call | solution.py:200
  75.5 11.0 %exchange.1 = f32[128,128]{1,0:T(8,128)} custom-call(f32[128,128]{1,0:T(8,128)} %bitcast.19), custom_call_target="tpu_custom_call" | custom-call | tf_op jit(solution)/shard_map/exchange/pallas_call | solution.py:243
  86.6 0.0 copy-start
  86.6 1.5 %reshape.24 = f32[2,8192]{1,0:T(2,128)} reshape(f32[128,128]{1,0:T(8,128)} %exchange.1) | data formatting | bytes 131072 | tf_op jit(solution)/shard_map/reshape | solution.py:296
  88.1 0.0 copy-done
  88.1 0.7 reshape.25
Async XLA Ops:
  1.6 1.2 %copy-start.1 = (s32[8192]{0:T(1024)S(1)}, s32[8192]{0:T(1024)}, u32[]{:S(2)}) copy-start(s32[8192]{0:T(1024)} %param.8) | copy-start | bytes 98308
  1.6 1.2 %copy-start.2 = (s32[8192]{0:T(1024)S(1)}, s32[8192]{0:T(1024)}, u32[]{:S(2)}) copy-start(s32[8192]{0:T(1024)} %param.5) | copy-start | bytes 98308
  86.6 1.6 %copy-start = (bf16[32,1024]{1,0:T(8,128)(2,1)S(1)}, bf16[32,1024]{1,0:T(8,128)(2,1)}, u32[]{:S(2)}) copy-start(bf16[32,1024]{1,0:T(8,128)(2,1)} %get-tuple-element.5) | copy-start | bytes 196612

commit v2 on v0

v2 whole, which is shorter than its diff:
```python
import functools

import jax
import jax.numpy as jnp
import numpy as np
from jax import lax
from jax.experimental import pallas as pl
from jax.experimental.pallas import tpu as pltpu
from jax.sharding import PartitionSpec as P

NX = 512
NY = 64
ZDEV = 4
STEPS = 2
TYPES = 2
SPREAD = 2

chi_mix = 1.0
kappa_comp = 0.5

MESH = pl.DeviceIdType.MESH
VMEM = pltpu.MemorySpace.VMEM
LIMIT = 60 * 1024 * 1024


def kernel_table():
    column = np.arange(NX, dtype=np.float32)
    distance = np.abs(column[:, None] - column[None, :])
    distance = np.minimum(distance, NX - distance)
    weights = np.exp(-distance * distance / np.float32(2.0 * SPREAD * SPREAD))
    return (weights / np.sum(weights[0])).astype(jnp.bfloat16)


def split_cell(cells):
    return cells % NX, cells // NX % NY, cells // (NX * NY)


def onehot(ids, size):
    tile = min(256, size)
    count = lax.broadcasted_iota(jnp.int32, (tile, ids.shape[1]), 0).astype(jnp.bfloat16)
    one = jnp.ones(count.shape, jnp.bfloat16)
    zero = jnp.zeros(count.shape, jnp.bfloat16)
    tiles = []
    for start in range(0, size, tile):
        here = jnp.broadcast_to((ids - start).astype(jnp.bfloat16), count.shape)
        tiles.append(jnp.where(count == here, one, zero))
    return jnp.concatenate(tiles, axis=0) if len(tiles) > 1 else tiles[0]


def fused_kernel(
    mol, grid, scale, cell_ref, move_ref, accept_ref, type_ref, table_ref,
    out_ref, own_ref,
    ids, total, count, inbox, fields, turned, part, inbox_e,
    send_a, recv_a, send_b, recv_b, send_e, recv_e,
):
    me = lax.axis_index("mol")
    slab = lax.axis_index("grid")
    beads = cell_ref.shape[1]
    blocks, block = part.shape[1], part.shape[3]
    planes = ZDEV * grid
    band = NY // mol
    half = count.shape[2] // 2

    barrier = pltpu.get_barrier_semaphore()
    for away in range(1, mol):
        pl.semaphore_signal(
            barrier, inc=1, device_id={"mol": lax.rem(me + away, mol)}, device_id_type=MESH
        )
    for away in range(1, grid):
        pl.semaphore_signal(
            barrier, inc=1, device_id={"grid": lax.rem(slab + away, grid)}, device_id_type=MESH
        )

    def window(index):
        return pl.ds(pl.multiple_of(index * block, block), block)

    def row_of(spot, kinds):
        _, row_y, plane_z = spot
        row = ((row_y // band * TYPES + kinds) * band + row_y % band) * ZDEV + plane_z % ZDEV
        return jnp.where(plane_z // ZDEV == slab, row, -1)

    def wrap(value, length):
        value = jnp.where(value < 0, value + length, value)
        return jnp.where(value >= length, value - length, value)

    def prepare(index, carry):
        here = window(index)
        kinds = type_ref[:, here]
        position = split_cell(cell_ref[:, here])
        for step in range(STEPS):
            lengths = (NX, NY, planes)
            proposed = tuple(
                wrap(position[i] + move_ref[step, i : i + 1, here], lengths[i]) for i in range(3)
            )
            ids[4 * step, :, here] = row_of(position, kinds)
            ids[4 * step + 1, :, here] = position[0]
            ids[4 * step + 2, :, here] = row_of(proposed, kinds)
            ids[4 * step + 3, :, here] = proposed[0]
            taken = accept_ref[step : step + 1, here] == 1
            position = tuple(jnp.where(taken, proposed[i], position[i]) for i in range(3))
        return carry

    lax.fori_loop(0, blocks, prepare, 0)

    def deposit(step, begin, end):
        def add(index, carry):
            here = window(index)
            rows = onehot(ids[4 * step, :, here], total.shape[0])
            cols = onehot(ids[4 * step + 1, :, here], total.shape[1])
            total[...] += lax.dot_general(
                rows, cols, (((1,), (1,)), ((), ())), preferred_element_type=jnp.float32
            )
            return carry

        if begin == 0:
            total[...] = jnp.zeros_like(total)
        lax.fori_loop(begin, end, add, 0)
        if end == blocks:
            count[step] = total[...].astype(jnp.bfloat16).reshape(count.shape[1:])

    def copy_a(step, away):
        to = lax.rem(me + away, mol)
        return pltpu.make_async_remote_copy(
            src_ref=count.at[step, to],
            dst_ref=inbox.at[step, away - 1],
            send_sem=send_a.at[step, away - 1],
            recv_sem=recv_a.at[step, away - 1],
            device_id={"mol": to},
            device_id_type=MESH,
        )

    def copy_b(step, away):
        return pltpu.make_async_remote_copy(
            src_ref=fields.at[step, me],
            dst_ref=fields.at[step, me],
            send_sem=send_b.at[step, away - 1],
            recv_sem=recv_b.at[step, away - 1],
            device_id={"mol": lax.rem(me + away, mol)},
            device_id_type=MESH,
        )

    def copy_e(step, index, away):
        return pltpu.make_async_remote_copy(
            src_ref=part.at[step, index],
            dst_ref=inbox_e.at[away - 1, step, index],
            send_sem=send_e.at[step, index, away - 1],
            recv_sem=recv_e.at[step, index, away - 1],
            device_id={"grid": lax.rem(slab + away, grid)},
            device_id_type=MESH,
        )

    def make_field(step):
        summed = count[step, me].astype(jnp.float32)
        for away in range(1, mol):
            copy_a(step, away).wait_recv()
            summed = summed + inbox[step, away - 1].astype(jnp.float32)
        high = summed.astype(jnp.bfloat16)
        low = (summed - high.astype(jnp.float32)).astype(jnp.bfloat16)
        table = table_ref[...]
        density = jnp.dot(high, table, preferred_element_type=jnp.float32)
        density = scale * (density + jnp.dot(low, table, preferred_element_type=jnp.float32))
        phi_a, phi_b = density[:half], density[half:]
        excess = kappa_comp * (phi_a + phi_b - 1.0)
        field_a = (chi_mix * phi_b + excess).astype(jnp.bfloat16)
        field_b = (chi_mix * phi_a + excess).astype(jnp.bfloat16)
        fields[step, me, :half] = field_a
        fields[step, me, half:] = field_b
        for away in range(1, mol):
            copy_b(step, away).start()
        if step == STEPS - 1:
            own_ref[:, :NX] = field_a
            own_ref[:, NX:] = field_b

    def turn(step):
        for away in range(1, mol):
            copy_b(step, away).wait_recv()
        eye = (
            lax.broadcasted_iota(jnp.int32, (NX, NX), 0)
            == lax.broadcasted_iota(jnp.int32, (NX, NX), 1)
        )
        eye = jnp.where(eye, 1.0, 0.0).astype(jnp.bfloat16)
        flat = fields[step].reshape(turned.shape[1], NX)
        turned[...] = lax.dot_general(
            eye, flat, (((1,), (1,)), ((), ())), preferred_element_type=jnp.float32
        ).astype(jnp.bfloat16)

    def pick(rows, cols):
        table = turned[...]
        values = jnp.dot(table, onehot(rows, table.shape[1]), preferred_element_type=jnp.float32)
        columns = lax.broadcasted_iota(jnp.int32, values.shape, 0)
        return jnp.sum(jnp.where(columns == cols, values, 0.0), axis=0, keepdims=True)

    def read(step, begin, end):
        def look(index, carry):
            here = window(index)
            old = pick(ids[4 * step, :, here], ids[4 * step + 1, :, here])
            new = pick(ids[4 * step + 2, :, here], ids[4 * step + 3, :, here])
            part[step, index] = new - old
            for away in range(1, grid):
                copy_e(step, index, away).start()
            return carry

        lax.fori_loop(begin, end, look, 0)

    deposit(0, 0, blocks)
    pl.semaphore_wait(barrier, mol - 1 + grid - 1)
    for away in range(1, mol):
        copy_a(0, away).start()
    early = blocks * 3 // 4
    deposit(1, 0, early)
    make_field(0)
    deposit(1, early, blocks)
    for away in range(1, mol):
        copy_a(1, away).start()
    turn(0)
    middle = blocks // 2
    read(0, 0, middle)
    make_field(1)
    read(0, middle, blocks)
    turn(1)
    read(1, 0, blocks)

    for step in range(STEPS):
        def settle(index, carry):
            energy = part[step, index]
            for away in range(1, grid):
                copy_e(step, index, away).wait_recv()
                energy = energy + inbox_e[away - 1, step, index]
            out_ref[step : step + 1, window(index)] = energy
            return carry

        lax.fori_loop(0, blocks, settle, 0)
    for step in range(STEPS):
        for away in range(1, mol):
            copy_a(step, away).wait_send()
            copy_b(step, away).wait_send()

        def drain(index, carry):
            for away in range(1, grid):
                copy_e(step, index, away).wait_send()
            return carry

        lax.fori_loop(0, blocks, drain, 0)


def local(cells_start, moves, accepted, bead_types):
    grid = lax.axis_size("grid")
    mol = lax.axis_size("mol")
    planes = ZDEV * grid
    beads = cells_start.shape[0]
    scale = NX * NY * planes / (beads * mol)
    band = NY // mol
    row_total = TYPES * NY * ZDEV
    rows = row_total // mol
    block = min(1024, beads)
    blocks = beads // block
    spec = pl.BlockSpec(memory_space=VMEM)
    bf16, f32 = jnp.bfloat16, jnp.float32
    dma = pltpu.SemaphoreType.DMA
    total, own = pl.pallas_call(
        functools.partial(fused_kernel, mol, grid, scale),
        out_shape=[
            jax.ShapeDtypeStruct((STEPS, beads), f32),
            jax.ShapeDtypeStruct((band * ZDEV, TYPES * NX), bf16),
        ],
        in_specs=[spec] * 5,
        out_specs=[spec] * 2,
        scratch_shapes=[
            pltpu.VMEM((4 * STEPS, 1, beads), jnp.int32),
            pltpu.VMEM((row_total, NX), f32),
            pltpu.VMEM((STEPS, mol, rows, NX), bf16),
            pltpu.VMEM((STEPS, mol - 1, rows, NX), bf16),
            pltpu.VMEM((STEPS, mol, rows, NX), bf16),
            pltpu.VMEM((NX, row_total), bf16),
            pltpu.VMEM((STEPS, blocks, 1, block), f32),
            pltpu.VMEM((grid - 1, STEPS, blocks, 1, block), f32),
            dma((STEPS, mol - 1)),
            dma((STEPS, mol - 1)),
            dma((STEPS, mol - 1)),
            dma((STEPS, mol - 1)),
            dma((STEPS, blocks, grid - 1)),
            dma((STEPS, blocks, grid - 1)),
        ],
        compiler_params=pltpu.CompilerParams(
            collective_id=0, has_side_effects=True, vmem_limit_bytes=LIMIT
        ),
        name="chain",
    )(
        cells_start.reshape(1, beads), moves, accepted,
        bead_types.reshape(1, beads), jnp.asarray(kernel_table()),
    )
    return total, own.reshape(band, ZDEV, TYPES * NX)


def solution(mesh):
    return jax.shard_map(
        local,
        mesh=mesh,
        in_specs=(P("mol"), P(None, None, "mol"), P(None, "mol"), P("mol")),
        out_specs=(P(None, "mol"), P("mol", "grid", None)),
        check_vma=False,
    )
```

time: 395 us -> 61.6 us (0.16)
  local copies, waits for them, and re-layouts: 212 us -> 3.92 us
  Pallas kernels: 0 us -> 56.9 us
  waiting for transfers between devices: 55.8 us -> 0 us
  other arithmetic: 53.9 us -> 0 us
  matrix products: 29 us -> 0 us
  blocking collectives: 28.4 us -> 0 us
  between operations: 14 us -> 0.65 us
    gather x4 -> x0, local copies, waits for them, and re-layouts: 202 us -> none  [read_beads(): picked = jnp.take(flat_table, flat_index).astype(jnp.float32)]
    pallas_call x0 -> x1, Pallas kernels: none -> 56.9 us  [local(): pl.pallas_call(functools.partial(fused_kernel, mol, grid, scale), out_sha...]
    reduce_scatter x1 -> x0, waiting for transfers between devices: 43.9 us -> none  [local(): lax.psum_scatter(both_terms(jnp.int32(0)), 'mol', scatter_dimension=0, ti...]
    select_n x20 -> x0, other arithmetic: 32 us -> none  [the longest x16 30.1 us: add_block(): first = jnp.where(types_here[:, None] == 0, spread_rows, zeros_bf)]
    dot_general x16 -> x0, matrix products: 29 us -> none  [add_block(): return total + jnp.dot(onehot, columns, preferred_element_type=jnp.float32)]
    all_gather x2 -> x0, blocking collectives: 28.4 us -> none  [local(): whole_z = lax.all_gather(fields[step], 'grid', axis=1, tiled=True)]
    all_gather x2 -> x0, waiting for transfers between devices: 11.8 us -> none  [local(): lax.all_gather(whole_z, 'mol', axis=0, tiled=True)]
    reduce_sum x16 -> x0, other arithmetic: 10.5 us -> none  [kernel_rows(): total = jnp.sum(jnp.exp(-first * first / (2.0 * SPREAD * SPREAD)))]
  transfers between devices with their start and end apart: 3 -> 0, of which waited for: 2 -> 0; matrix products, arithmetic and copies ran while one was open for 27% -> 0% of each run, Pallas kernels for 0% -> 0%
where the time goes in v2:
time: 61.6 us; the launch traced here: 61.4 us
  Pallas kernels  56.9 us (92%)
  local copies, waits for them, and re-layouts  3.92 us (6%)
  between operations  0.65 us (1%)
    pallas_call x1, Pallas kernels, local(): pl.pallas_call(functools.partial(fused_kernel, mol, grid, scale), out_sha...  56.9 us
    unnamed x4, local copies, waits for them, and re-layouts  2.39 us
    reshape x1, local copies, waits for them, and re-layouts, local(): return (total, own.reshape(band, ZDEV, TYPES * NX))  1.53 us

profile of v2, /device:TPU:0, one launch (start us, length us, event | category | flops | bytes accessed | tf_op | source)
XLA Modules:
  0.0 61.4 jit_solution(9110352992896506975)
XLA Ops:
  0.6 1.8 %copy.7.move_ref = s32[2,3,8192]{2,1,0:T(4,128)} copy(s32[2,3,8192]{2,0,1:T(2,128)} %param.6) | data formatting | bytes 393216 | tf_op args[1]
  2.4 56.9 %chain.1 = (f32[2,8192]{1,0:T(2,128)}, bf16[32,1024]{1,0:T(8,128)(2,1)}) custom-call(s32[1,8192]{1,0:T(1,128)} %bitcast.2, s32[2,3,8192]{2,1,0:T(4,128)} %copy.7.move_ref, s32[2,8192]{1,0:T(2,128)} %accept_ref.1, s32[1,8192]{1,0:T(1,128)} %bitcast.3, bf16[512,512]{1,0:T(8,128)(2,1)} %constant.2.clone.table_ref), custom_call_target="tpu_custom_call" | custom-call | tf_op jit(solution)/shard_map/chain/pallas_call | solution.py:260
  59.2 0.0 copy-start
  59.3 1.5 %reshape.15 = bf16[8,4,1024]{2,1,0:T(4,128)(2,1)} reshape(bf16[32,1024]{1,0:T(8,128)(2,1)} %get-tuple-element.5) | data formatting | bytes 131072 | tf_op jit(solution)/shard_map/reshape | solution.py:292
  60.8 0.0 copy-done
  60.8 0.6 %copy.9 = f32[2,8192]{1,0:T(2,128)} copy(f32[2,8192]{1,0:T(2,128)S(1)} %copy-done) | data formatting | bytes 131072
Async XLA Ops:
  59.2 1.5 %copy-start = (f32[2,8192]{1,0:T(2,128)S(1)}, f32[2,8192]{1,0:T(2,128)}, u32[]{:S(2)}) copy-start(f32[2,8192]{1,0:T(2,128)} %get-tuple-element.8) | copy-start | bytes 196612

commit v3 on v2

--- a/solution.py
+++ b/solution.py
@@ -31,8 +31,16 @@
     return (weights / np.sum(weights[0])).astype(jnp.bfloat16)
 
 
+def divide(value, size):
+    if size & (size - 1) == 0:
+        return value >> (size.bit_length() - 1), value & (size - 1)
+    return value // size, value % size
+
+
 def split_cell(cells):
-    return cells % NX, cells // NX % NY, cells // (NX * NY)
+    rest, col_x = divide(cells, NX)
+    plane_z, row_y = divide(rest, NY)
+    return col_x, row_y, plane_z
 
 
 def onehot(ids, size):
@@ -76,12 +84,21 @@
 
     def row_of(spot, kinds):
         _, row_y, plane_z = spot
-        row = ((row_y // band * TYPES + kinds) * band + row_y % band) * ZDEV + plane_z % ZDEV
-        return jnp.where(plane_z // ZDEV == slab, row, -1)
+        owner, row_here = divide(row_y, band)
+        owner_z, plane_here = divide(plane_z, ZDEV)
+        row = ((owner * TYPES + kinds) * band + row_here) * ZDEV + plane_here
+        return jnp.where(owner_z == slab, row, -1)
 
     def wrap(value, length):
         value = jnp.where(value < 0, value + length, value)
         return jnp.where(value >= length, value - length, value)
+
+    def begin_ids(index, carry):
+        here = window(index)
+        position = split_cell(cell_ref[:, here])
+        ids[0, :, here] = row_of(position, type_ref[:, here])
+        ids[1, :, here] = position[0]
+        return carry
 
     def prepare(index, carry):
         here = window(index)
@@ -90,23 +107,24 @@
         for step in range(STEPS):
             lengths = (NX, NY, planes)
             proposed = tuple(
-                wrap(position[i] + move_ref[step, i : i + 1, here], lengths[i]) for i in range(3)
+                wrap(position[i] + move_ref[i, step : step + 1, here], lengths[i]) for i in range(3)
             )
-            ids[4 * step, :, here] = row_of(position, kinds)
-            ids[4 * step + 1, :, here] = position[0]
+            if step > 0:
+                ids[4 * step, :, here] = row_of(position, kinds)
+                ids[4 * step + 1, :, here] = position[0]
             ids[4 * step + 2, :, here] = row_of(proposed, kinds)
             ids[4 * step + 3, :, here] = proposed[0]
             taken = accept_ref[step : step + 1, here] == 1
             position = tuple(jnp.where(taken, proposed[i], position[i]) for i in range(3))
         return carry
 
-    lax.fori_loop(0, blocks, prepare, 0)
+    lax.fori_loop(0, blocks, begin_ids, 0)
 
     def deposit(step, begin, end):
         def add(index, carry):
             here = window(index)
-            rows = onehot(ids[4 * step, :, here], total.shape[0])
-            cols = onehot(ids[4 * step + 1, :, here], total.shape[1])
+            rows = onehot(ids[4 * step, :, here], total.shape[0]).astype(jnp.float8_e4m3fn)
+            cols = onehot(ids[4 * step + 1, :, here], total.shape[1]).astype(jnp.float8_e4m3fn)
             total[...] += lax.dot_general(
                 rows, cols, (((1,), (1,)), ((), ())), preferred_element_type=jnp.float32
             )
@@ -129,15 +147,29 @@
             device_id_type=MESH,
         )
 
-    def copy_b(step, away):
+    partner = me + 1 - 2 * lax.rem(me, 2)
+    chips = mol // 2
+
+    def copy_b(step, index):
+        if index == 0:
+            slot, to = me, partner
+        elif index < chips:
+            slot, to = me, lax.rem(me + 2 * index, mol)
+        else:
+            slot, to = lax.rem(me + mol - 2 * (index - chips + 1), mol), partner
         return pltpu.make_async_remote_copy(
-            src_ref=fields.at[step, me],
-            dst_ref=fields.at[step, me],
-            send_sem=send_b.at[step, away - 1],
-            recv_sem=recv_b.at[step, away - 1],
-            device_id={"mol": lax.rem(me + away, mol)},
+            src_ref=fields.at[step, slot],
+            dst_ref=fields.at[step, slot],
+            send_sem=send_b.at[step, index],
+            recv_sem=recv_b.at[step, index],
+            device_id={"mol": to},
             device_id_type=MESH,
         )
+
+    def forward(step):
+        for index in range(1, chips):
+            copy_b(step, index).wait_recv()
+            copy_b(step, index + chips - 1).start()
 
     def copy_e(step, index, away):
         return pltpu.make_async_remote_copy(
@@ -161,19 +193,21 @@
         density = scale * (density + jnp.dot(low, table, preferred_element_type=jnp.float32))
         phi_a, phi_b = density[:half], density[half:]
         excess = kappa_comp * (phi_a + phi_b - 1.0)
-        field_a = (chi_mix * phi_b + excess).astype(jnp.bfloat16)
-        field_b = (chi_mix * phi_a + excess).astype(jnp.bfloat16)
-        fields[step, me, :half] = field_a
-        fields[step, me, half:] = field_b
-        for away in range(1, mol):
-            copy_b(step, away).start()
+        wide_a = chi_mix * phi_b + excess
+        wide_b = chi_mix * phi_a + excess
+        fields[step, me, :half] = wide_a.astype(jnp.bfloat16)
+        fields[step, me, half:] = wide_b.astype(jnp.bfloat16)
+        for index in reversed(range(chips)):
+            copy_b(step, index).start()
         if step == STEPS - 1:
-            own_ref[:, :NX] = field_a
-            own_ref[:, NX:] = field_b
+            for row in range(band):
+                here = slice(row * ZDEV, (row + 1) * ZDEV)
+                own_ref[row, :, :NX] = wide_a[here].astype(jnp.bfloat16)
+                own_ref[row, :, NX:] = wide_b[here].astype(jnp.bfloat16)
 
     def turn(step):
-        for away in range(1, mol):
-            copy_b(step, away).wait_recv()
+        for index in [0, *range(chips, 2 * chips - 1)]:
+            copy_b(step, index).wait_recv()
         eye = (
             lax.broadcasted_iota(jnp.int32, (NX, NX), 0)
             == lax.broadcasted_iota(jnp.int32, (NX, NX), 1)
@@ -206,17 +240,19 @@
     pl.semaphore_wait(barrier, mol - 1 + grid - 1)
     for away in range(1, mol):
         copy_a(0, away).start()
-    early = blocks * 3 // 4
-    deposit(1, 0, early)
+    lax.fori_loop(0, blocks, prepare, 0)
+    deposit(1, 0, blocks)
     make_field(0)
-    deposit(1, early, blocks)
     for away in range(1, mol):
         copy_a(1, away).start()
+    forward(0)
     turn(0)
-    middle = blocks // 2
+    middle, late = blocks // 2, blocks * 3 // 4
     read(0, 0, middle)
     make_field(1)
-    read(0, middle, blocks)
+    read(0, middle, late)
+    forward(1)
+    read(0, late, blocks)
     turn(1)
     read(1, 0, blocks)
 
@@ -233,7 +269,7 @@
     for step in range(STEPS):
         for away in range(1, mol):
             copy_a(step, away).wait_send()
-            copy_b(step, away).wait_send()
+            copy_b(step, away - 1).wait_send()
 
         def drain(index, carry):
             for away in range(1, grid):
@@ -252,7 +288,7 @@
     band = NY // mol
     row_total = TYPES * NY * ZDEV
     rows = row_total // mol
-    block = min(1024, beads)
+    block = min(2048, beads)
     blocks = beads // block
     spec = pl.BlockSpec(memory_space=VMEM)
     bf16, f32 = jnp.bfloat16, jnp.float32
@@ -261,7 +297,7 @@
         functools.partial(fused_kernel, mol, grid, scale),
         out_shape=[
             jax.ShapeDtypeStruct((STEPS, beads), f32),
-            jax.ShapeDtypeStruct((band * ZDEV, TYPES * NX), bf16),
+            jax.ShapeDtypeStruct((band, ZDEV, TYPES * NX), bf16),
         ],
         in_specs=[spec] * 5,
         out_specs=[spec] * 2,
@@ -286,10 +322,10 @@
         ),
         name="chain",
     )(
-        cells_start.reshape(1, beads), moves, accepted,
+        cells_start.reshape(1, beads), moves.transpose(1, 0, 2), accepted,
         bead_types.reshape(1, beads), jnp.asarray(kernel_table()),
     )
-    return total, own.reshape(band, ZDEV, TYPES * NX)
+    return total, own
 
 
 def solution(mesh):

time: 61.6 us -> 54.9 us (0.89)
  Pallas kernels: 56.9 us -> 52 us
  local copies, waits for them, and re-layouts: 3.92 us -> 2.14 us
    pallas_call x1, Pallas kernels: 56.9 us -> 52 us  [local(): pl.pallas_call(functools.partial(fused_kernel, mol, grid, scale), out_sha...]
    reshape x1 -> x0, local copies, waits for them, and re-layouts: 1.53 us -> none  [local(): return (total, own.reshape(band, ZDEV, TYPES * NX))]
where the time goes in v3:
time: 54.9 us; the launch traced here: 54.8 us
  Pallas kernels  52 us (95%)
  local copies, waits for them, and re-layouts  2.14 us (4%)
  between operations  0.65 us (1%)
    pallas_call x1, Pallas kernels, local(): pl.pallas_call(functools.partial(fused_kernel, mol, grid, scale), out_sha...  52 us
    unnamed x4, local copies, waits for them, and re-layouts  2.14 us

profile of v3, /device:TPU:0, one launch (start us, length us, event | category | flops | bytes accessed | tf_op | source)
XLA Modules:
  0.0 54.8 jit_solution(8513358114743796105)
XLA Ops:
  0.6 52.0 %chain.1 = (f32[2,8192]{1,0:T(2,128)}, bf16[8,4,1024]{2,1,0:T(4,128)(2,1)}) custom-call(s32[1,8192]{1,0:T(1,128)} %bitcast.4, s32[3,2,8192]{2,1,0:T(2,128)} %bitcast.3, s32[2,8192]{1,0:T(2,128)} %accept_ref.1, s32[1,8192]{1,0:T(1,128)} %bitcast.5, bf16[512,512]{1,0:T(8,128)(2,1)} %constant.2.clone.table_ref), custom_call_target="tpu_custom_call" | custom-call | tf_op jit(solution)/shard_map/chain/pallas_call | solution.py:296
  52.6 0.0 copy-start
  52.6 1.5 %copy.9 = f32[2,8192]{1,0:T(2,128)} copy(f32[2,8192]{1,0:T(2,128)} %get-tuple-element.4) | data formatting | bytes 131072
  54.1 0.0 copy-done
  54.1 0.6 %copy.10 = bf16[8,4,1024]{2,1,0:T(4,128)(2,1)} copy(bf16[8,4,1024]{2,1,0:T(4,128)(2,1)S(1)} %copy-done) | data formatting | bytes 131072
Async XLA Ops:
  52.6 1.5 %copy-start = (bf16[8,4,1024]{2,1,0:T(4,128)(2,1)S(1)}, bf16[8,4,1024]{2,1,0:T(4,128)(2,1)}, u32[]{:S(2)}) copy-start(bf16[8,4,1024]{2,1,0:T(4,128)(2,1)} %get-tuple-element.5) | copy-start | bytes 196612

commit v4 on v3

--- a/solution.py
+++ b/solution.py
@@ -247,7 +247,7 @@
         copy_a(1, away).start()
     forward(0)
     turn(0)
-    middle, late = blocks // 2, blocks * 3 // 4
+    middle, late = blocks // 4, blocks * 3 // 4
     read(0, 0, middle)
     make_field(1)
     read(0, middle, late)

time: 54.9 us -> 54 us (0.984)
  Pallas kernels: 52 us -> 51 us
    pallas_call x1, Pallas kernels: 52 us -> 51 us  [local(): pl.pallas_call(functools.partial(fused_kernel, mol, grid, scale), out_sha...]
where the time goes in v4:
time: 54 us; the launch traced here: 53.8 us
  Pallas kernels  51 us (94%)
  local copies, waits for them, and re-layouts  2.14 us (4%)
  between operations  0.65 us (1%)
    pallas_call x1, Pallas kernels, local(): pl.pallas_call(functools.partial(fused_kernel, mol, grid, scale), out_sha...  51 us
    unnamed x4, local copies, waits for them, and re-layouts  2.14 us

profile of v4, /device:TPU:0, one launch (start us, length us, event | category | flops | bytes accessed | tf_op | source)
XLA Modules:
  0.0 53.8 jit_solution(8019184277562839163)
XLA Ops:
  0.6 51.0 %chain.1 = (f32[2,8192]{1,0:T(2,128)}, bf16[8,4,1024]{2,1,0:T(4,128)(2,1)}) custom-call(s32[1,8192]{1,0:T(1,128)} %bitcast.4, s32[3,2,8192]{2,1,0:T(2,128)} %bitcast.3, s32[2,8192]{1,0:T(2,128)} %accept_ref.1, s32[1,8192]{1,0:T(1,128)} %bitcast.5, bf16[512,512]{1,0:T(8,128)(2,1)} %constant.2.clone.table_ref), custom_call_target="tpu_custom_call" | custom-call | tf_op jit(solution)/shard_map/chain/pallas_call | solution.py:296
  51.6 0.0 copy-start
  51.6 1.5 %copy.9 = f32[2,8192]{1,0:T(2,128)} copy(f32[2,8192]{1,0:T(2,128)} %get-tuple-element.4) | data formatting | bytes 131072
  53.1 0.0 copy-done
  53.1 0.6 %copy.10 = bf16[8,4,1024]{2,1,0:T(4,128)(2,1)} copy(bf16[8,4,1024]{2,1,0:T(4,128)(2,1)S(1)} %copy-done) | data formatting | bytes 131072
Async XLA Ops:
  51.6 1.5 %copy-start = (bf16[8,4,1024]{2,1,0:T(4,128)(2,1)S(1)}, bf16[8,4,1024]{2,1,0:T(4,128)(2,1)}, u32[]{:S(2)}) copy-start(bf16[8,4,1024]{2,1,0:T(4,128)(2,1)} %get-tuple-element.5) | copy-start | bytes 196612
